TPU v7x, 32 devices: a whole 2x2x4 slice. The times are simulated.
32 devices in a mesh: dp: 4 (over z), mp: 8 (over y, x, core).
Axes of the slice: x: 2, y: 2, z: 4, core: 2. Of those that a mesh axis runs over, the one named last changes fastest.
Arguments:
- grad_parts: bfloat16 [4, 8, 2, 18432, 128], P('dp', 'mp'), may hold values from -45 to 45
- master: float32 [8, 2, 18432, 128], P('mp', None, 'dp'), may hold values from -15 to 15
- momenta: float32 [3, 8, 2, 18432, 128], P(None, 'mp', None, 'dp'), may hold values from -45 to 45
- second: float32 [3, 8, 2, 18432, 128], P(None, 'mp', None, 'dp'), may hold values from 0.00025 to 330
- step_count: int32 [1], replicated, may hold values from 1 to 99999
- mlp_first: float32 [8, 4], replicated, may hold values from -2 to 2
- mlp_bias: float32 [4], replicated, may hold values from -3 to 3
- mlp_second: float32 [4, 2], replicated, may hold values from -3 to 3
- tensor_weight: float32 [10], replicated, may hold values from -2 to 2
Outputs:
- new_params: bfloat16 [8, 2, 18432, 128], P('mp')
- new_master: float32 [8, 2, 18432, 128], P('mp', None, 'dp')
- new_momenta: float32 [3, 8, 2, 18432, 128], P(None, 'mp', None, 'dp')
- new_second: float32 [3, 8, 2, 18432, 128], P(None, 'mp', None, 'dp')
- update: float32 [8, 2, 18432, 128], P('mp', None, 'dp')
All inputs are finite; a program needn't handle non-finite values.
Results may differ from a plain program's by a relative error of at most 0.019.
Values may be sent and summed in bfloat16 or wider, within the bound.
A program may use at most 192 MiB of HBM per device.

v0:
```python
import jax
import jax.numpy as jnp
from jax import lax
from jax.sharding import PartitionSpec as P

D = 4608
HQ = 4096
RATES = (0.9, 0.99, 0.999)


def advance(gradient, momenta, second):
    moments = jnp.stack(
        [rate * momenta[i] + (1.0 - rate) * gradient for i, rate in enumerate(RATES)]
    )
    squares = jnp.stack(
        [rate * second[i] + (1.0 - rate) * gradient * gradient for i, rate in enumerate(RATES)]
    )
    return (moments, squares)


def features_of(master, gradient, moments, squares):
    listing = [master, gradient, moments[0], moments[1], moments[2]]
    for slot_id in range(3):
        listing.append(moments[slot_id] / jnp.sqrt(squares[slot_id]))
    return listing


def perceptron(normed, boost, mlp_first, mlp_bias, mlp_second):
    direction = jnp.zeros_like(normed[0])
    magnitude = jnp.zeros_like(normed[0])
    for unit_id in range(mlp_first.shape[1]):
        active = mlp_first[0, unit_id] * normed[0]
        for feat_id in range(1, len(normed)):
            active = active + mlp_first[feat_id, unit_id] * normed[feat_id]
        active = jax.nn.relu(active + mlp_bias[unit_id])
        direction = direction + mlp_second[unit_id, 0] * active
        magnitude = magnitude + mlp_second[unit_id, 1] * active
    return direction * jnp.exp(0.5 * jnp.tanh(magnitude)) * boost


def tensor_boost(norms, step_count, tensor_weight):
    count = tensor_weight.shape[0] - 2
    step_value = step_count[0].astype(jnp.float32)
    first_phase = jnp.log1p(step_value) / 11.5
    second_phase = step_value / 100000.0
    logits = jnp.sum(tensor_weight[:count, None] * jnp.log(norms), axis=0)
    logits = logits + tensor_weight[count] * first_phase + tensor_weight[count + 1] * second_phase
    return jnp.exp(jnp.tanh(logits))


def square_sums(listing):
    return jnp.stack([jnp.sum(feature * feature, axis=(0, 2, 3)) for feature in listing])


def local(
    grad_parts, master, momenta, second, step_count, mlp_first, mlp_bias, mlp_second, tensor_weight
):
    gradient = lax.psum_scatter(grad_parts, "dp", scatter_dimension=3, tiled=True).astype(
        jnp.float32
    )[0]
    new_momenta, new_second = advance(gradient, momenta, second)
    early_local = square_sums([master, gradient])
    listing = features_of(master, gradient, new_momenta, new_second)
    late_local = square_sums(listing[2:])
    totals = lax.psum(jnp.concatenate([early_local, late_local], axis=0), ("dp", "mp"))
    norms = jnp.sqrt(totals / float(D * HQ) + 1e-06)
    boost = tensor_boost(norms, step_count, tensor_weight)[None, :, None, None]
    normed = [listing[i] / norms[i][None, :, None, None] for i in range(len(listing))]
    update = perceptron(normed, boost, mlp_first, mlp_bias, mlp_second)
    new_master = master - 0.05 * update
    new_params = lax.all_gather(new_master.astype(jnp.bfloat16), "dp", axis=2, tiled=True)
    return (new_params, new_master, new_momenta, new_second, update)


def solution(mesh):
    placed = (
        P("dp", "mp", None, None, None),
        P("mp", None, "dp", None),
        P(None, "mp", None, "dp", None),
        P(None, "mp", None, "dp", None),
        P(),
        P(),
        P(),
        P(),
        P(),
    )
    return jax.shard_map(
        local,
        mesh=mesh,
        in_specs=placed,
        out_specs=(
            P("mp", None, None, None),
            P("mp", None, "dp", None),
            P(None, "mp", None, "dp", None),
            P(None, "mp", None, "dp", None),
            P("mp", None, "dp", None),
        ),
        check_vma=False,
    )
```

profile of v0, /device:TPU:0, one launch (start us, length us, event | category | flops | bytes accessed | tf_op | source)
XLA Modules:
  0.0 466.4 jit_solution(5703901997524263589)
XLA Ops:
  7.2 0.7 reduce-scatter.2.cloned.1.call-update
  8.7 3.0 multiply_reduce_fusion.6
  11.7 0.1 copy.22
  11.8 0.6 fusion.33
  13.1 0.6 fusion.32
  13.7 0.7 fusion.31
  14.4 0.7 fusion.30
  15.1 0.7 fusion.29
  15.9 158.4 %reduce-scatter.2.cloned.1.call-done = bf16[1,1,2,4608,128]{4,3,2,1,0:T(8,128)(2,1)} async-done(((bf16[1,1,2,18432,128]{4,3,2,1,0:T(8,128)(2,1)}), bf16[1,1,2,4608,128]{4,3,2,1,0:T(8,128)(2,1)}) %reduce-scatter.2.cloned.1.call-update) | async-done | bytes 2359312 | tf_op jit(solution)/shard_map/reduce_scatter | solution.py:58
  174.3 14.4 %multiply_reduce_fusion = (f32[2]{0:T(128)S(1)}, f32[2]{0:T(128)S(1)}, f32[2]{0:T(128)S(1)}, f32[2]{0:T(128)S(1)}, f32[2]{0:T(128)S(1)}, /*index=5*/f32[2]{0:T(128)S(1)}, f32[2]{0:T(128)S(1)}) fusion(bf16[1,1,2,4608,128]{4,3,2,1,0:T(8,128)(2,1)} %reduce-scatter.2.cloned.1.call-done, f32[3,1,2,4608,128]{4,3,2,1,0:T(8,128)} %param.12, ...), kind=kLoop, calls=%fused_computation.38 | loop fusion | flops 42467320 | bytes 30670904 | tf_op jit(solution)/shard_map/reduce_sum | solution.py:52
  188.7 0.1 copy.27
  188.8 0.1 copy.29
  188.9 0.1 copy.28
  189.0 0.1 copy.24
  189.2 0.1 copy.26
  189.3 0.1 concatenate.3
  190.1 41.2 %psum.7 = f32[8,2]{0,1:T(2,128)S(1)} all-reduce(f32[8,2]{0,1:T(2,128)S(1)} %concatenate.3), channel_id=1, replica_groups=mesh['dp'=4,'mp'=8] {'dp','mp'}, use_global_device_ids=true, to_apply=%region_9.0 | all-reduce | flops 16 | bytes 128 | tf_op jit(solution)/shard_map/psum | solution.py:65
  231.3 0.1 fusion.27
  231.4 0.3 slice_reduce_fusion.7
  231.7 52.0 %fusion.28 = (bf16[1,2,4608,128]{3,2,1,0:T(8,128)(2,1)}, f32[1,2,4608,128]{3,2,1,0:T(8,128)}, f32[1,2,4608,128]{3,2,1,0:T(8,128)}) fusion(f32[1,2,4608,128]{3,2,1,0:T(8,128)} %param.10, f32[2]{0:T(128)S(1)} %tanh_exponential_fusion, f32[]{:T(128)} %bitcast.58, f32[]{:T(128)} %bitcast.57, f32[]{:T(128)} %bitcast.56, f32[]{:T(128)} %bitcast.55, f32[]{:T(128)} %bitcast.54, ...), kind=kLoop, calls=%fused_computation.64 | loop fusion | flops 139198464 | bytes 47186168 | tf_op jit(solution)/shard_map/convert_element_type | solution.py:71
  283.7 20.3 %fusion.24 = (f32[1,1,2,4608,128]{4,3,2,1,0:T(8,128)}, f32[1,1,2,4608,128]{4,3,2,1,0:T(8,128)}, f32[1,1,2,4608,128]{4,3,2,1,0:T(8,128)}, f32[1,1,2,4608,128]{4,3...) fusion(bf16[1,1,2,4608,128]{4,3,2,1,0:T(8,128)(2,1)S(1)} %copy-done, ...), kind=kLoop, calls=%fused_computation.33 | loop fusion | flops 22413312 | bytes 58982400 | tf_op jit(solution)/shard_map/add | solution.py:16
  304.1 18.9 %pad_maximum_fusion = (f32[3,1,2,4608,128]{4,3,2,1,0:T(8,128)}, f32[3,1,2,4608,128]{4,3,2,1,0:T(8,128)}) fusion(f32[1,1,2,4608,128]{4,3,2,1,0:T(8,128)} %get-tuple-element.29, f32[1,1,2,4608,128]{4,3,2,1,0:T(8,128)} %get-tuple-element.30, f32[1,1,2,4608,128]{4,3,2,1,0:T(8,128)} %get-tuple-element.31, f32[1,1,2,4608,128]{4,3,2,1,0:T(8,128)} %get-tuple-element.25, ...), kind=kLoop, calls=%fused_computation | loop fusion | flops 14155776 | bytes 56623104 | tf_op jit(solution)/shard_map/stack | solution.py:12
  323.0 127.5 %all-gather.2.cloned.1.call-done = bf16[1,2,18432,128]{3,2,1,0:T(8,128)(2,1)} async-done(((bf16[1,2,4608,128]{3,2,1,0:T(8,128)(2,1)}), bf16[1,2,18432,128]{3,2,1,0:T(8,128)(2,1)}) %all-gather.2.cloned.1.call-update) | async-done | bytes 9437200 | tf_op jit(solution)/shard_map/all_gather | solution.py:71
  450.4 9.1 %copy.32 = bf16[1,2,18432,128]{3,2,1,0:T(8,128)(2,1)} copy(bf16[1,2,18432,128]{3,2,1,0:T(8,128)(2,1)} %all-gather.2.cloned.1.call-done) | data formatting | bytes 18874368
  (17 shorter events, 0.3 us)
Async XLA Ops:
  7.2 167.1 %reduce-scatter.2.cloned.1.call-start = ((), (), s32[]{:S(2)}) async-start(), calls=%async_computation.1 | async-start | bytes 11796480 | tf_op jit(solution)/shard_map/reduce_scatter | solution.py:58
  7.9 3.9 copy-start.4
  7.9 5.1 %copy-start.3 = (f32[4]{0:T(128)S(1)}, f32[4]{0:T(128)}, u32[]{:S(2)}) copy-start(f32[4]{0:T(128)} %param.15) | copy-start | bytes 52
  7.9 5.8 %copy-start.2 = (f32[4,2]{0,1:T(2,128)S(1)}, f32[4,2]{0,1:T(2,128)}, u32[]{:S(2)}) copy-start(f32[4,2]{0,1:T(2,128)} %param.16) | copy-start | bytes 100
  7.9 6.5 %copy-start.1 = (f32[8,4]{0,1:T(4,128)S(1)}, f32[8,4]{0,1:T(4,128)}, u32[]{:S(2)}) copy-start(f32[8,4]{0,1:T(4,128)} %param.14) | copy-start | bytes 388
  7.9 442.5 %all-gather.2.cloned.1.call-start = ((), (), s32[]{:S(2)}) async-start(), calls=%async_computation.2 | async-start | bytes 11796480 | tf_op jit(solution)/shard_map/all_gather | solution.py:71
  174.3 57.4 %copy-start = (bf16[1,1,2,4608,128]{4,3,2,1,0:T(8,128)(2,1)S(1)}, bf16[1,1,2,4608,128]{4,3,2,1,0:T(8,128)(2,1)}, u32[]{:S(2)}) copy-start(bf16[1,1,2,4608,128]{4,3,2,1,0:T(8,128)(2,1)} %reduce-scatter.2.cloned.1.call-done) | copy-start | bytes 7077892
Sparse Core Ops, SparseCore 0:
  10.3 163.9 reduce-scatter.1
  283.9 166.5 all-gather.1
where the time goes:
time: 467 us; the launch traced here: 466 us
  waiting for transfers between devices  287 us (61%)
  other arithmetic  109 us (23%)
  blocking collectives  41.2 us (9%)
  between operations  16.1 us (3%)
  local copies, waits for them, and re-layouts  13.6 us (3%)
    reduce_scatter x1, waiting for transfers between devices, local(): lax.psum_scatter(grad_parts, 'dp', scatter_dimension=3, tiled=True)  158 us
    all_gather x1, waiting for transfers between devices, local(): lax.all_gather(new_master.astype(jnp.bfloat16), 'dp', axis=2, tiled=True)  127 us
    convert_element_type x1, other arithmetic, local(): new_master.astype(jnp.bfloat16)  52 us
    psum x1, blocking collectives, local(): lax.psum(jnp.concatenate([early_local, late_local], axis=0), ('dp', 'mp'))  41.2 us
    add x1, other arithmetic, advance(): rate * second[i] + (1.0 - rate) * gradient * gradient  20.3 us
    another operation x1, other arithmetic, advance(): jnp.stack([rate * momenta[i] + (1.0 - rate) * gradient for i, rate in enu...  18.9 us
    reduce_sum x2, other arithmetic, square_sums(): jnp.sum(feature * feature, axis=(0, 2, 3))  17.4 us
  transfers between devices with their start and end apart: 2, of which 2 were waited for; matrix products, arithmetic and copies ran while one was open for 10% of the time, Pallas kernels for 0%

commit v1 on v0

--- a/solution.py
+++ b/solution.py
@@ -68,7 +68,12 @@
     normed = [listing[i] / norms[i][None, :, None, None] for i in range(len(listing))]
     update = perceptron(normed, boost, mlp_first, mlp_bias, mlp_second)
     new_master = master - 0.05 * update
-    new_params = lax.all_gather(new_master.astype(jnp.bfloat16), "dp", axis=2, tiled=True)
+    new_params = jnp.concatenate(
+        lax.all_to_all(
+            jnp.stack([new_master.astype(jnp.bfloat16)] * lax.axis_size("dp")), "dp", 0, 0
+        ),
+        axis=2,
+    )
     return (new_params, new_master, new_momenta, new_second, update)
 
 

time: 467 us -> 515 us (1.10)
  waiting for transfers between devices: 287 us -> 326 us
  starting transfers between devices: 0.08 us -> 6.03 us
    all_to_all x0 -> x1, waiting for transfers between devices: none -> 167 us  [local(): lax.all_to_all(jnp.stack([new_master.astype(jnp.bfloat16)] * lax.axis_siz...]
    all_gather x1 -> x0, waiting for transfers between devices: 127 us -> none  [local(): lax.all_gather(new_master.astype(jnp.bfloat16), 'dp', axis=2, tiled=True)]
    unnamed x11 -> x10, local copies, waits for them, and re-layouts: 9.14 us -> 0.02 us
    all_to_all x0 -> x1, local copies, waits for them, and re-layouts: none -> 8.1 us  [local(): lax.all_to_all(jnp.stack([new_master.astype(jnp.bfloat16)] * lax.axis_siz...]
    all_to_all x0 -> x1, starting transfers between devices: none -> 5.99 us  [local(): lax.all_to_all(jnp.stack([new_master.astype(jnp.bfloat16)] * lax.axis_siz...]
  transfers between devices with their start and end apart: 2 -> 2, of which waited for: 2 -> 2; matrix products, arithmetic and copies ran while one was open for 10% -> 9% of each run, Pallas kernels for 0% -> 0%
where the time goes in v1:
time: 515 us; the launch traced here: 514 us
  waiting for transfers between devices  326 us (63%)
  other arithmetic  108 us (21%)
  blocking collectives  41.2 us (8%)
  local copies, waits for them, and re-layouts  17.6 us (3%)
  between operations  16.1 us (3%)
  starting transfers between devices  6.03 us (1%)
    all_to_all x1, waiting for transfers between devices, local(): lax.all_to_all(jnp.stack([new_master.astype(jnp.bfloat16)] * lax.axis_siz...  167 us
    reduce_scatter x1, waiting for transfers between devices, local(): lax.psum_scatter(grad_parts, 'dp', scatter_dimension=3, tiled=True)  158 us
    convert_element_type x1, other arithmetic, local(): new_master.astype(jnp.bfloat16)  51.7 us
    psum x1, blocking collectives, local(): lax.psum(jnp.concatenate([early_local, late_local], axis=0), ('dp', 'mp'))  41.2 us
    add x1, other arithmetic, advance(): rate * second[i] + (1.0 - rate) * gradient * gradient  19.7 us
    another operation x1, other arithmetic, advance(): jnp.stack([rate * momenta[i] + (1.0 - rate) * gradient for i, rate in enu...  18.6 us
    reduce_sum x2, other arithmetic, square_sums(): jnp.sum(feature * feature, axis=(0, 2, 3))  17.4 us
  transfers between devices with their start and end apart: 2, of which 2 were waited for; matrix products, arithmetic and copies ran while one was open for 9% of the time, Pallas kernels for 0%

profile of v1, /device:TPU:0, one launch (start us, length us, event | category | flops | bytes accessed | tf_op | source)
XLA Modules:
  0.0 514.1 jit_solution(8666093548195073739)
XLA Ops:
  7.2 0.7 reduce-scatter.2.cloned.1.call-update
  8.7 3.0 multiply_reduce_fusion.6
  11.7 0.1 copy.22
  11.8 0.6 fusion.32
  13.1 0.6 fusion.31
  13.7 0.7 fusion.30
  14.4 0.7 fusion.29
  15.1 0.7 fusion.28
  15.8 158.4 %reduce-scatter.2.cloned.1.call-done = bf16[1,1,2,4608,128]{4,3,2,1,0:T(8,128)(2,1)} async-done(((bf16[1,1,2,18432,128]{4,3,2,1,0:T(8,128)(2,1)}), bf16[1,1,2,4608,128]{4,3,2,1,0:T(8,128)(2,1)}) %reduce-scatter.2.cloned.1.call-update) | async-done | bytes 2359312 | tf_op jit(solution)/shard_map/reduce_scatter | solution.py:58
  174.3 14.4 %multiply_reduce_fusion = (f32[2]{0:T(128)S(1)}, f32[2]{0:T(128)S(1)}, f32[2]{0:T(128)S(1)}, f32[2]{0:T(128)S(1)}, f32[2]{0:T(128)S(1)}, /*index=5*/f32[2]{0:T(128)S(1)}, f32[2]{0:T(128)S(1)}) fusion(bf16[1,1,2,4608,128]{4,3,2,1,0:T(8,128)(2,1)} %reduce-scatter.2.cloned.1.call-done, f32[3,1,2,4608,128]{4,3,2,1,0:T(8,128)} %param.12, ...), kind=kLoop, calls=%fused_computation.38 | loop fusion | flops 42467320 | bytes 30670904 | tf_op jit(solution)/shard_map/reduce_sum | solution.py:52
  188.7 0.1 copy.27
  188.8 0.1 copy.29
  189.2 0.1 copy.26
  189.3 0.1 concatenate.3
  190.1 41.2 %psum.7 = f32[8,2]{0,1:T(2,128)S(1)} all-reduce(f32[8,2]{0,1:T(2,128)S(1)} %concatenate.3), channel_id=1, replica_groups=mesh['dp'=4,'mp'=8] {'dp','mp'}, use_global_device_ids=true, to_apply=%region_9.0 | all-reduce | flops 16 | bytes 128 | tf_op jit(solution)/shard_map/psum | solution.py:65
  231.3 0.1 fusion.27
  231.4 0.3 slice_reduce_fusion.7
  231.7 51.7 %convert_bitcast_fusion.1 = (bf16[2,4608,128]{2,1,0:T(8,128)(2,1)S(1)}, f32[1,2,4608,128]{3,2,1,0:T(8,128)}, f32[1,2,4608,128]{3,2,1,0:T(8,128)}) fusion(f32[1,2,4608,128]{3,2,1,0:T(8,128)} %param.10, f32[2]{0:T(128)S(1)} %tanh_exponential_fusion, f32[]{:T(128)} %bitcast.58, f32[]{:T(128)} %bitcast.57, f32[]{:T(128)} %bitcast.56, f32[]{:T(128)} %bitcast.55, ...), kind=kLoop, calls=%fused_computation.51 | loop fusion | flops 139198464 | bytes 47186168 | tf_op jit(solution)/shard_map/convert_element_type | solution.py:73
  283.4 5.0 stack.51
  288.4 6.0 %all-to-all-start = ((bf16[4,1,2,4608,128]{4,3,2,1,0:T(8,128)(2,1)}), bf16[4,1,2,4608,128]{4,3,2,1,0:T(8,128)(2,1)}, u32[]{:S(2)}, u32[]{:S(2)}) async-start(bf16[4,1,2,4608,128]{4,3,2,1,0:T(8,128)(2,1)} %stack.51), calls=%async_computation.1 | async-start | bytes 18874368 | tf_op jit(solution)/shard_map/all_to_all | solution.py:72
  294.4 19.7 %fusion.24 = (f32[1,1,2,4608,128]{4,3,2,1,0:T(8,128)}, f32[1,1,2,4608,128]{4,3,2,1,0:T(8,128)}, f32[1,1,2,4608,128]{4,3,2,1,0:T(8,128)}, f32[1,1,2,4608,128]{4,3...) fusion(bf16[1,1,2,4608,128]{4,3,2,1,0:T(8,128)(2,1)S(1)} %copy-done, ...), kind=kLoop, calls=%fused_computation.33 | loop fusion | flops 22413312 | bytes 58982400 | tf_op jit(solution)/shard_map/add | solution.py:16
  314.1 18.6 %pad_maximum_fusion = (f32[3,1,2,4608,128]{4,3,2,1,0:T(8,128)}, f32[3,1,2,4608,128]{4,3,2,1,0:T(8,128)}) fusion(f32[1,1,2,4608,128]{4,3,2,1,0:T(8,128)} %get-tuple-element.29, f32[1,1,2,4608,128]{4,3,2,1,0:T(8,128)} %get-tuple-element.30, f32[1,1,2,4608,128]{4,3,2,1,0:T(8,128)} %get-tuple-element.31, f32[1,1,2,4608,128]{4,3,2,1,0:T(8,128)} %get-tuple-element.25, ...), kind=kLoop, calls=%fused_computation | loop fusion | flops 14155776 | bytes 56623104 | tf_op jit(solution)/shard_map/stack | solution.py:12
  332.6 166.6 %all-to-all-done = bf16[4,1,2,4608,128]{4,3,2,1,0:T(8,128)(2,1)} async-done(((bf16[4,1,2,4608,128]{4,3,2,1,0:T(8,128)(2,1)}), bf16[4,1,2,4608,128]{4,3,2,1,0:T(8,128)(2,1)}, u32[]{:S(2)}, u32[]{:S(2)}) %all-to-all-start) | async-done | bytes 9437216 | tf_op jit(solution)/shard_map/all_to_all | solution.py:72
  499.2 8.1 %copy.30 = bf16[4,1,2,4608,128]{4,3,0,2,1:T(8,128)(2,1)} copy(bf16[4,1,2,4608,128]{4,3,2,1,0:T(8,128)(2,1)} %all-to-all-done) | data formatting | bytes 18874368 | tf_op jit(solution)/shard_map/all_to_all | solution.py:72
  (17 shorter events, 0.4 us)
Async XLA Ops:
  7.2 167.1 %reduce-scatter.2.cloned.1.call-start = ((), (), s32[]{:S(2)}) async-start(), calls=%async_computation.2 | async-start | bytes 11796480 | tf_op jit(solution)/shard_map/reduce_scatter | solution.py:58
  7.9 3.9 copy-start.4
  7.9 5.1 copy-start.3
  7.9 5.8 %copy-start.2 = (f32[4,2]{0,1:T(2,128)S(1)}, f32[4,2]{0,1:T(2,128)}, u32[]{:S(2)}) copy-start(f32[4,2]{0,1:T(2,128)} %param.16) | copy-start | bytes 100
  7.9 6.5 %copy-start.1 = (f32[8,4]{0,1:T(4,128)S(1)}, f32[8,4]{0,1:T(4,128)}, u32[]{:S(2)}) copy-start(f32[8,4]{0,1:T(4,128)} %param.14) | copy-start | bytes 388
  174.3 57.4 %copy-start = (bf16[1,1,2,4608,128]{4,3,2,1,0:T(8,128)(2,1)S(1)}, bf16[1,1,2,4608,128]{4,3,2,1,0:T(8,128)(2,1)}, u32[]{:S(2)}) copy-start(bf16[1,1,2,4608,128]{4,3,2,1,0:T(8,128)(2,1)} %reduce-scatter.2.cloned.1.call-done) | copy-start | bytes 7077892
  288.4 210.8 %all-to-all-start = ((bf16[4,1,2,4608,128]{4,3,2,1,0:T(8,128)(2,1)}), bf16[4,1,2,4608,128]{4,3,2,1,0:T(8,128)(2,1)}, u32[]{:S(2)}, u32[]{:S(2)}) async-start(bf16[4,1,2,4608,128]{4,3,2,1,0:T(8,128)(2,1)} %stack.51), calls=%async_computation.1 | async-start | bytes 18874368 | tf_op jit(solution)/shard_map/all_to_all | solution.py:72
Sparse Core Ops, SparseCore 0:
  10.3 163.9 reduce-scatter.1
